TPU v7x, 32 devices: a whole 2x2x4 slice. The times are simulated.
32 devices in a mesh: tmpl: 2 (over core), row: 4 (over z), col: 4 (over y, x).
Axes of the slice: x: 2, y: 2, z: 4, core: 2. Of those that a mesh axis runs over, the one named last changes fastest.
Arguments:
- template_pair: bfloat16 [2, 512, 64, 512], P('tmpl', 'row', None, 'col'), may hold values from -6 to 6
- trunk: bfloat16 [512, 128, 512], P('row', None, 'col'), may hold values from -6 to 6
- coverage: int32 [2, 512], replicated, may hold values from 0 to 1, as said below
- chain_ids: int32 [512], replicated, may hold values from 0 to 3, never falling along the last dimension, each value on 1 to 256 neighbouring positions
- chain_vec: float32 [64], replicated, may hold values from -4 to 4
- trunk_weights: bfloat16 [64, 128], replicated, may hold values from -0.5 to 0.5
- proj_weights: bfloat16 [2, 5, 64, 64], replicated, may hold values from -0.75 to 0.75
- out_weights: bfloat16 [2, 64, 64], replicated, may hold values from -0.75 to 0.75
- final_weights: bfloat16 [128, 64], replicated, may hold values from -0.75 to 0.75
Outputs:
- trunk_out: bfloat16 [512, 128, 512], P('row', None, 'col')
Inputs may be any that keep to these rules, and one draw needn't show every extreme that they name: coverage[t, i] is 1 where template t covers token i, else 0; how densely a template covers tokens is drawn anew for each block of 128 consecutive tokens. `chain_ids`: chain ids never fall along the tokens.
All inputs are finite; a program needn't handle non-finite values.
Results may differ from a plain program's by a relative error of at most 0.008.
Values may be sent and summed in bfloat16 or wider, within the bound.
No kernel may reach another device: no remote copies, remote signals or barrier semaphores. Data moves between devices by JAX's collectives and lax.ppermute only.
A program may use at most 128 MiB of HBM per device.

v0:
```python
import jax
import jax.numpy as jnp
from jax import lax
from jax.sharding import PartitionSpec as P

epsilon = 1e-05


def from_root(block, axis, source):
    block = jnp.where(lax.axis_index(axis) == source, block, jnp.zeros_like(block))
    return lax.psum(block, axis)


def channel_norm(values):
    centre = jnp.mean(values, axis=1, keepdims=True)
    centred = values - centre
    spread = jnp.mean(centred * centred, axis=1, keepdims=True)
    return centred * lax.rsqrt(spread + epsilon)


def project(weights, values):
    return jnp.einsum("dc,icj->idj", weights, values, preferred_element_type=jnp.float32)


def rounded(values):
    return lax.optimization_barrier(values.astype(jnp.bfloat16)).astype(jnp.float32)


def gated_pair(pair_rep, pair_mask, weights):
    channels = pair_rep.shape[1]
    normed = channel_norm(pair_rep.astype(jnp.float32)).astype(jnp.bfloat16)
    stacked = project(weights.reshape(5 * channels, channels), normed)
    pieces = [stacked[:, number * channels : (number + 1) * channels, :] for number in range(5)]
    weighted = pair_mask[:, None, :]
    left_proj = (weighted * jax.nn.sigmoid(pieces[0]) * pieces[1]).astype(jnp.bfloat16)
    right_proj = (weighted * jax.nn.sigmoid(pieces[2]) * pieces[3]).astype(jnp.bfloat16)
    return (left_proj, right_proj, pieces[4])


def apply_update(pair_rep, tri_sum, gate_proj, weights):
    tri_norm = channel_norm(tri_sum).astype(jnp.bfloat16)
    update = jax.nn.sigmoid(gate_proj) * project(weights, tri_norm)
    return (pair_rep.astype(jnp.float32) + update).astype(jnp.bfloat16)


def outgoing(left_proj, right_proj):
    right_cols = lax.all_gather(right_proj, "row", axis=0, tiled=True)
    partial_value = jnp.einsum(
        "ick,jck->icj", left_proj, right_cols, preferred_element_type=jnp.float32
    )
    return lax.psum_scatter(
        partial_value.astype(jnp.bfloat16), "col", scatter_dimension=2, tiled=True
    ).astype(jnp.float32)


def incoming(left_proj, right_proj):
    tile_rows, channels, tile_cols = left_proj.shape
    row_devices = lax.axis_size("row")
    owners = row_devices // lax.axis_size("col")
    left_cols, right_cols = (
        lax.all_gather(left_proj, "row", axis=0, tiled=True),
        lax.all_gather(right_proj, "row", axis=0, tiled=True),
    )
    offset = lax.axis_index("row") % owners * tile_rows
    column_piece = lax.dynamic_slice_in_dim(left_cols, offset, tile_rows, 2)
    left_mine = from_root(column_piece, "col", lax.axis_index("row") // owners)
    left_split = left_mine.reshape(row_devices, tile_rows, channels, tile_rows)
    right_split = right_cols.reshape(row_devices, tile_rows, channels, tile_cols)
    blocks = jnp.einsum(
        "gkci,gkcj->gicj", left_split, right_split, preferred_element_type=jnp.float32
    )
    return jnp.sum(rounded(blocks), axis=0)


def finish(trunk, pooled, cover_count, final_weights):
    hidden = jax.nn.relu(pooled / jnp.maximum(cover_count, 1.0)[:, None, :]).astype(jnp.bfloat16)
    return (trunk.astype(jnp.float32) + project(final_weights, hidden)).astype(jnp.bfloat16)


def per_device(
    template_pair,
    trunk,
    coverage,
    chain_ids,
    chain_vec,
    trunk_weights,
    proj_weights,
    out_weights,
    final_weights,
):
    tile_rows, trunk_channels, tile_cols = trunk.shape
    row_start = lax.axis_index("row") * tile_rows
    col_start = lax.axis_index("col") * tile_cols
    cover_float = coverage.astype(jnp.float32)
    cover_rows = lax.dynamic_slice_in_dim(cover_float, row_start, tile_rows, 1)
    cover_cols = lax.dynamic_slice_in_dim(cover_float, col_start, tile_cols, 1)
    cover_count = jnp.sum(cover_rows[:, :, None] * cover_cols[:, None, :], axis=0)
    chain_rows = lax.dynamic_slice_in_dim(chain_ids, row_start, tile_rows, 0)
    chain_cols = lax.dynamic_slice_in_dim(chain_ids, col_start, tile_cols, 0)
    same_chain = (chain_rows[:, None] == chain_cols[None, :]).astype(jnp.float32)
    trunk_proj = project(trunk_weights, channel_norm(trunk.astype(jnp.float32)))
    local_templates = template_pair.shape[0]
    template_index = lax.axis_index("tmpl") * local_templates + 0
    mask_rows = lax.dynamic_index_in_dim(cover_rows, template_index, 0, keepdims=False)
    mask_cols = lax.dynamic_index_in_dim(cover_cols, template_index, 0, keepdims=False)
    pair_mask = mask_rows[:, None] * mask_cols[None, :]
    pair_rep = (
        template_pair[0].astype(jnp.float32)
        + same_chain[:, None, :] * chain_vec[None, :, None]
        + trunk_proj
    ).astype(jnp.bfloat16)
    left_proj, right_proj, gate_proj = gated_pair(pair_rep, pair_mask, proj_weights[0])
    pair_rep = apply_update(pair_rep, outgoing(left_proj, right_proj), gate_proj, out_weights[0])
    left_proj, right_proj, gate_proj = gated_pair(pair_rep, pair_mask, proj_weights[1])
    pair_rep = apply_update(pair_rep, incoming(left_proj, right_proj), gate_proj, out_weights[1])
    pooled = pair_mask[:, None, :] * channel_norm(pair_rep.astype(jnp.float32))
    pooled_all = lax.psum(pooled.astype(jnp.bfloat16), "tmpl").astype(jnp.float32)
    return finish(trunk, pooled_all, cover_count, final_weights)


def solution(mesh):
    in_specs = (
        P("tmpl", "row", None, "col"),
        P("row", None, "col"),
        P(),
        P(),
        P(),
        P(),
        P(),
        P(),
        P(),
    )
    out_specs = P("row", None, "col")
    return jax.shard_map(
        per_device, mesh=mesh, in_specs=in_specs, out_specs=out_specs, check_vma=False
    )
```

profile of v0, /device:TPU:0, one launch (start us, length us, event | category | flops | bytes accessed | tf_op | source)
XLA Modules:
  0.0 877.8 jit_solution(267695753060939710)
XLA Ops:
  7.4 6.4 copy.107
  17.3 4.8 fusion.2
  22.2 6.3 convert_reduce_fusion.4
  29.6 8.5 convolution_bitcast_fusion.1
  38.3 8.4 fusion.47
  47.3 151.9 %all-gather.4.cloned.1.call-done = bf16[512,64,128]{2,1,0:T(8,128)(2,1)} async-done(((bf16[128,64,128]{2,1,0:T(8,128)(2,1)}), bf16[512,64,128]{2,1,0:T(8,128)(2,1)}) %all-gather.4.cloned.1.call-update) | async-done | bytes 8388624 | tf_op jit(solution)/shard_map/all_gather | solution.py:47
  199.2 15.7 %convert_bitcast_fusion.1 = bf16[128,64,512]{0,2,1:T(8,128)(2,1)} fusion(bf16[512,64,128]{2,1,0:T(8,128)(2,1)} %all-gather.4.cloned.1.call-done, bf16[128,64,128]{2,1,0:T(8,128)(2,1)S(1)} %get-tuple-element.9), kind=kOutput, calls=%fused_computation.17 | convolution fusion | flops 1077936128 | bytes 18874368 | tf_op jit(solution)/shard_map/ick,jck->icj/dot_general | solution.py:48
  215.1 84.4 %reduce-scatter.2.cloned.1.call-done = bf16[128,64,128]{0,2,1:T(8,128)(2,1)} async-done(((bf16[128,64,512]{0,2,1:T(8,128)(2,1)}), bf16[128,64,128]{0,2,1:T(8,128)(2,1)}) %reduce-scatter.2.cloned.1.call-update) | async-done | bytes 2097168 | tf_op jit(solution)/shard_map/reduce_scatter | solution.py:51
  306.2 4.3 copy.116
  310.5 4.8 convert_reduce_fusion.3
  319.3 4.4 fusion.38
  328.4 148.9 %all-gather.8.cloned.1.call-done = bf16[512,64,128]{2,1,0:T(8,128)(2,1)} async-done(((bf16[128,64,128]{2,1,0:T(8,128)(2,1)}), bf16[512,64,128]{2,1,0:T(8,128)(2,1)}) %all-gather.8.cloned.1.call-update) | async-done | bytes 8388624 | tf_op jit(solution)/shard_map/all_gather | solution.py:61
  477.3 7.4 broadcast_select_fusion
  484.7 12.9 %copy.118 = bf16[4,128,64,128]{3,1,2,0:T(8,128)(2,1)} copy(bf16[4,128,64,128]{3,2,1,0:T(8,128)(2,1)} %bitcast.56) | data formatting | bytes 16777216 | tf_op jit(solution)/shard_map/reshape | solution.py:67
  497.9 128.6 %all-gather.6.cloned.1.call-done = bf16[512,64,128]{2,1,0:T(8,128)(2,1)} async-done(((bf16[128,64,128]{2,1,0:T(8,128)(2,1)}), bf16[512,64,128]{2,1,0:T(8,128)(2,1)}) %all-gather.6.cloned.1.call-update) | async-done | bytes 8388624 | tf_op jit(solution)/shard_map/all_gather | solution.py:62
  626.5 173.6 %all-reduce.3.cloned.1.call-done = bf16[4,128,64,128]{3,1,2,0:T(8,128)(2,1)} async-done(((bf16[4,128,64,128]{3,1,2,0:T(8,128)(2,1)}), bf16[4,128,64,128]{3,1,2,0:T(8,128)(2,1)}) %all-reduce.3.cloned.1.call-update) | async-done | bytes 8388624 | tf_op jit(solution)/shard_map/psum | solution.py:11
  800.2 10.6 %convert_bitcast_fusion = bf16[4,128,64,128]{1,3,2,0:T(8,128)(2,1)S(1)} fusion(bf16[4,128,64,128]{3,1,2,0:T(8,128)(2,1)} %all-reduce.3.cloned.1.call-done, bf16[4,128,64,128]{3,2,1,0:T(8,128)(2,1)} %bitcast.57), kind=kOutput, calls=%fused_computation.16 | convolution fusion | flops 1077936128 | bytes 25165824 | tf_op jit(solution)/shard_map/gkci,gkcj->gicj/dot_general | solution.py:69
  810.7 5.0 convert_reduce_fusion
  818.8 4.4 multiply_convert_fusion
  823.2 4.4 copy.124
  827.6 4.8 convert_reduce_fusion.5
  835.9 22.0 %all-reduce.5.cloned.1.call-done = bf16[128,64,128]{2,1,0:T(8,128)(2,1)} async-done(((bf16[128,64,128]{2,1,0:T(8,128)(2,1)}), bf16[128,64,128]{2,1,0:T(8,128)(2,1)}) %all-reduce.5.cloned.1.call-update) | async-done | bytes 2097168 | tf_op jit(solution)/shard_map/psum | solution.py:117
  857.9 6.2 fusion.5
  864.1 6.4 copy.125
  (79 shorter events, 28.3 us)
Async XLA Ops:
  6.5 851.4 %copy-start = (bf16[128,64]{0,1:T(8,128)(2,1)S(1)}, bf16[128,64]{0,1:T(8,128)(2,1)}, u32[]{:S(2)}) copy-start(bf16[128,64]{0,1:T(8,128)(2,1)} %param.17) | copy-start | bytes 49156
  6.5 192.7 %all-gather.4.cloned.1.call-start = ((), (), s32[]{:S(2)}) async-start(), calls=%async_computation.1 | async-start | bytes 10485760 | tf_op jit(solution)/shard_map/all_gather | solution.py:47
  13.7 3.5 copy-start.2
  13.7 8.4 copy-start.10
  13.7 8.5 copy-start.12
  13.7 8.5 copy-start.13
  22.2 7.3 copy-start.8
  22.2 7.3 copy-start.9
  28.5 9.5 %copy-start.4 = (bf16[128,64,128]{2,1,0:T(8,128)(2,1)}, bf16[128,64,128]{2,1,0:T(8,128)(2,1)S(1)}, u32[]{:S(2)}) copy-start(bf16[128,64,128]{2,1,0:T(8,128)(2,1)S(1)} %get-tuple-element.20) | copy-start | bytes 6291460
  46.7 252.9 %reduce-scatter.2.cloned.1.call-start = ((), (), s32[]{:S(2)}) async-start(), calls=%async_computation.2 | async-start | bytes 10485760 | tf_op jit(solution)/shard_map/reduce_scatter | solution.py:51
  214.9 262.4 %all-gather.8.cloned.1.call-start = ((), (), s32[]{:S(2)}) async-start(), calls=%async_computation.4 | async-start | bytes 10485760 | tf_op jit(solution)/shard_map/all_gather | solution.py:61
  299.6 4.6 copy-start.3
  304.2 6.3 copy-start.11
  306.2 4.3 copy-start.5
  315.3 3.9 copy-start.6
  319.3 8.2 copy-start.1
  327.5 299.0 %all-gather.6.cloned.1.call-start = ((), (), s32[]{:S(2)}) async-start(), calls=%async_computation.3 | async-start | bytes 10485760 | tf_op jit(solution)/shard_map/all_gather | solution.py:62
  328.1 472.1 %all-reduce.3.cloned.1.call-start = ((), (), s32[]{:S(2)}) async-start(), calls=%async_computation.5 | async-start | bytes 16777216 | tf_op jit(solution)/shard_map/psum | solution.py:11
  497.6 360.3 %all-reduce.5.cloned.1.call-start = ((), (), s32[]{:S(2)}) async-start(), calls=%async_computation.6 | async-start | bytes 4194304 | tf_op jit(solution)/shard_map/psum | solution.py:117
  818.8 8.8 %copy-start.7 = (bf16[128,64,128]{2,1,0:T(8,128)(2,1)S(1)}, bf16[128,64,128]{2,1,0:T(8,128)(2,1)}, u32[]{:S(2)}) copy-start(bf16[128,64,128]{2,1,0:T(8,128)(2,1)} %copy-done.6) | copy-start | bytes 6291460
Sparse Core Ops, SparseCore 0:
  46.8 152.3 all-gather.3
  215.0 84.4 reduce-scatter.1
  327.7 149.5 all-gather.7
  478.7 147.7 all-gather.5
  629.9 170.2 all-reduce.2
  835.9 21.9 all-reduce.4
where the time goes:
time: 884 us; the launch traced here: 878 us
  waiting for transfers between devices  710 us (80%)
  matrix products  59.8 us (7%)
  other arithmetic  52.4 us (6%)
  local copies, waits for them, and re-layouts  39.8 us (5%)
  between operations  14.4 us (2%)
    psum x1, waiting for transfers between devices, from_root(): return lax.psum(block, axis)  174 us
    all_gather x1, waiting for transfers between devices, outgoing(): right_cols = lax.all_gather(right_proj, 'row', axis=0, tiled=True)  152 us
    all_gather x1, waiting for transfers between devices, incoming(): lax.all_gather(left_proj, 'row', axis=0, tiled=True)  149 us
    all_gather x1, waiting for transfers between devices, incoming(): lax.all_gather(right_proj, 'row', axis=0, tiled=True)  129 us
    reduce_scatter x1, waiting for transfers between devices, outgoing(): lax.psum_scatter(partial_value.astype(jnp.bfloat16), 'col', scatter_dimen...  84.4 us
    dot_general x6, matrix products, project(): jnp.einsum('dc,icj->idj', weights, values, preferred_element_type=jnp.flo...  33.5 us
    psum x1, waiting for transfers between devices, per_device(): lax.psum(pooled.astype(jnp.bfloat16), 'tmpl').astype(jnp.float32)  22 us
  transfers between devices with their start and end apart: 6, of which 6 were waited for; matrix products, arithmetic and copies ran while one was open for 2% of the time, Pallas kernels for 0%

commit v1 on v0

--- a/solution.py
+++ b/solution.py
@@ -8,7 +8,7 @@
 
 def from_root(block, axis, source):
     block = jnp.where(lax.axis_index(axis) == source, block, jnp.zeros_like(block))
-    return lax.psum(block, axis)
+    return jnp.sum(lax.all_gather(block, axis), axis=0)
 
 
 def channel_norm(values):

time: 884 us -> 1020 us (1.15)
  waiting for transfers between devices: 710 us -> 834 us
  other arithmetic: 52.4 us -> 69.9 us
  local copies, waits for them, and re-layouts: 39.8 us -> 26.7 us
    all_gather x0 -> x1, waiting for transfers between devices: none -> 294 us  [from_root(): return jnp.sum(lax.all_gather(block, axis), axis=0)]
    psum x1 -> x0, waiting for transfers between devices: 174 us -> none  [from_root(): return lax.psum(block, axis)]
    reduce_sum x0 -> x1, other arithmetic: none -> 17.9 us  [from_root(): return jnp.sum(lax.all_gather(block, axis), axis=0)]
    reshape x1 -> x0, local copies, waits for them, and re-layouts: 12.9 us -> none  [incoming(): left_split = left_mine.reshape(row_devices, tile_rows, channels, tile_rows)]
where the time goes in v1:
time: 1020 us; the launch traced here: 1010 us
  waiting for transfers between devices  834 us (82%)
  other arithmetic  69.9 us (7%)
  matrix products  67.8 us (7%)
  local copies, waits for them, and re-layouts  26.7 us (3%)
  between operations  14.3 us (1%)
    all_gather x1, waiting for transfers between devices, from_root(): return jnp.sum(lax.all_gather(block, axis), axis=0)  294 us
    all_gather x1, waiting for transfers between devices, outgoing(): right_cols = lax.all_gather(right_proj, 'row', axis=0, tiled=True)  152 us
    all_gather x1, waiting for transfers between devices, incoming(): lax.all_gather(left_proj, 'row', axis=0, tiled=True)  150 us
    all_gather x1, waiting for transfers between devices, incoming(): lax.all_gather(right_proj, 'row', axis=0, tiled=True)  133 us
    reduce_scatter x1, waiting for transfers between devices, outgoing(): lax.psum_scatter(partial_value.astype(jnp.bfloat16), 'col', scatter_dimen...  84.4 us
    dot_general x6, matrix products, project(): jnp.einsum('dc,icj->idj', weights, values, preferred_element_type=jnp.flo...  33.5 us
  transfers between devices with their start and end apart: 6, of which 6 were waited for; matrix products, arithmetic and copies ran while one was open for 2% of the time, Pallas kernels for 0%

profile of v1, /device:TPU:0, one launch (start us, length us, event | category | flops | bytes accessed | tf_op | source)
XLA Modules:
  0.0 1013.7 jit_solution(5860931529723378268)
XLA Ops:
  7.4 6.4 copy.107
  17.3 4.8 fusion.2
  22.2 6.3 convert_reduce_fusion.4
  29.6 8.5 convolution_bitcast_fusion.1
  38.3 8.4 fusion.50
  47.2 152.0 %all-gather.6.cloned.1.call-done = bf16[512,64,128]{2,1,0:T(8,128)(2,1)} async-done(((bf16[128,64,128]{2,1,0:T(8,128)(2,1)}), bf16[512,64,128]{2,1,0:T(8,128)(2,1)}) %all-gather.6.cloned.1.call-update) | async-done | bytes 8388624 | tf_op jit(solution)/shard_map/all_gather | solution.py:47
  199.2 15.7 %convert_bitcast_fusion.1 = bf16[128,64,512]{0,2,1:T(8,128)(2,1)} fusion(bf16[512,64,128]{2,1,0:T(8,128)(2,1)} %all-gather.6.cloned.1.call-done, bf16[128,64,128]{2,1,0:T(8,128)(2,1)S(1)} %get-tuple-element.9), kind=kOutput, calls=%fused_computation.18 | convolution fusion | flops 1077936128 | bytes 18874368 | tf_op jit(solution)/shard_map/ick,jck->icj/dot_general | solution.py:48
  215.1 84.4 %reduce-scatter.2.cloned.1.call-done = bf16[128,64,128]{0,2,1:T(8,128)(2,1)} async-done(((bf16[128,64,512]{0,2,1:T(8,128)(2,1)}), bf16[128,64,128]{0,2,1:T(8,128)(2,1)}) %reduce-scatter.2.cloned.1.call-update) | async-done | bytes 2097168 | tf_op jit(solution)/shard_map/reduce_scatter | solution.py:51
  306.2 4.3 copy.116
  310.5 4.8 convert_reduce_fusion.3
  319.3 4.4 fusion.41
  327.7 149.7 %all-gather.10.cloned.1.call-done = bf16[512,64,128]{2,1,0:T(8,128)(2,1)} async-done(((bf16[128,64,128]{2,1,0:T(8,128)(2,1)}), bf16[512,64,128]{2,1,0:T(8,128)(2,1)}) %all-gather.10.cloned.1.call-update) | async-done | bytes 8388624 | tf_op jit(solution)/shard_map/all_gather | solution.py:61
  477.3 7.1 broadcast_select_fusion
  485.4 294.5 %all-gather.12.cloned.1.call-done = bf16[2048,64,128]{2,1,0:T(8,128)(2,1)} async-done(((bf16[512,64,128]{2,1,0:T(8,128)(2,1)}), bf16[2048,64,128]{2,1,0:T(8,128)(2,1)}) %all-gather.12.cloned.1.call-update) | async-done | bytes 33554448 | tf_op jit(solution)/shard_map/all_gather | solution.py:11
  779.8 17.9 %reduce_sum.146 = bf16[512,64,128]{2,1,0:T(8,128)(2,1)} reduce(bf16[4,512,64,128]{3,2,1,0:T(8,128)(2,1)} %bitcast.56, bf16[]{:T(256)} %constant.93.clone.1), dimensions={0}, to_apply=%region_9.10 | reduce | flops 12582912 | bytes 41943040 | tf_op jit(solution)/shard_map/reduce_sum | solution.py:11
  797.7 133.2 %all-gather.8.cloned.1.call-done = bf16[512,64,128]{2,1,0:T(8,128)(2,1)} async-done(((bf16[128,64,128]{2,1,0:T(8,128)(2,1)}), bf16[512,64,128]{2,1,0:T(8,128)(2,1)}) %all-gather.8.cloned.1.call-update) | async-done | bytes 8388624 | tf_op jit(solution)/shard_map/all_gather | solution.py:62
  930.9 18.5 %convert_bitcast_fusion = bf16[4,128,64,128]{1,3,2,0:T(8,128)(2,1)S(1)} fusion(bf16[4,128,64,128]{3,2,1,0:T(8,128)(2,1)} %bitcast.57, bf16[4,128,64,128]{3,2,1,0:T(8,128)(2,1)} %bitcast.58), kind=kOutput, calls=%fused_computation.17 | convolution fusion | flops 1077936128 | bytes 25165824 | tf_op jit(solution)/shard_map/gkci,gkcj->gicj/dot_general | solution.py:69
  949.4 5.1 convert_reduce_fusion
  957.6 4.3 multiply_convert_fusion
  961.9 4.1 copy.124
  966.0 4.8 convert_reduce_fusion.5
  974.3 19.5 %all-reduce.2.cloned.1.call-done = bf16[128,64,128]{2,1,0:T(8,128)(2,1)} async-done(((bf16[128,64,128]{2,1,0:T(8,128)(2,1)}), bf16[128,64,128]{2,1,0:T(8,128)(2,1)}) %all-reduce.2.cloned.1.call-update) | async-done | bytes 2097168 | tf_op jit(solution)/shard_map/psum | solution.py:117
  993.8 6.2 fusion.5
  1000.1 6.4 copy.125
  (79 shorter events, 28.1 us)
Async XLA Ops:
  6.5 987.3 %copy-start = (bf16[128,64]{0,1:T(8,128)(2,1)S(1)}, bf16[128,64]{0,1:T(8,128)(2,1)}, u32[]{:S(2)}) copy-start(bf16[128,64]{0,1:T(8,128)(2,1)} %param.17) | copy-start | bytes 49156
  6.5 192.7 %all-gather.6.cloned.1.call-start = ((), (), s32[]{:S(2)}) async-start(), calls=%async_computation.1 | async-start | bytes 10485760 | tf_op jit(solution)/shard_map/all_gather | solution.py:47
  13.7 3.5 copy-start.2
  13.7 8.4 copy-start.10
  13.7 8.5 copy-start.12
  13.7 8.5 copy-start.13
  22.2 7.3 copy-start.8
  22.2 7.3 copy-start.9
  28.5 9.5 copy-start.4
  46.7 252.9 %reduce-scatter.2.cloned.1.call-start = ((), (), s32[]{:S(2)}) async-start(), calls=%async_computation.2 | async-start | bytes 10485760 | tf_op jit(solution)/shard_map/reduce_scatter | solution.py:51
  214.9 262.4 %all-gather.10.cloned.1.call-start = ((), (), s32[]{:S(2)}) async-start(), calls=%async_computation.4 | async-start | bytes 10485760 | tf_op jit(solution)/shard_map/all_gather | solution.py:61
  299.6 4.6 copy-start.3
  304.2 6.3 copy-start.11
  306.2 4.3 copy-start.5
  315.3 3.9 copy-start.6
  319.3 8.3 copy-start.1
  327.6 452.2 %all-gather.12.cloned.1.call-start = ((), (), s32[]{:S(2)}) async-start(), calls=%async_computation.6 | async-start | bytes 41943040 | tf_op jit(solution)/shard_map/all_gather | solution.py:11
  484.5 446.4 %all-gather.8.cloned.1.call-start = ((), (), s32[]{:S(2)}) async-start(), calls=%async_computation.3 | async-start | bytes 10485760 | tf_op jit(solution)/shard_map/all_gather | solution.py:62
  485.1 508.7 %all-reduce.2.cloned.1.call-start = ((), (), s32[]{:S(2)}) async-start(), calls=%async_computation.5 | async-start | bytes 4194304 | tf_op jit(solution)/shard_map/psum | solution.py:117
  957.6 8.5 copy-start.7
Sparse Core Ops, SparseCore 0:
  46.8 152.3 all-gather.5
  215.0 84.4 reduce-scatter.1
  327.7 149.5 all-gather.9
  484.6 295.1 all-gather.11
  781.2 149.5 all-gather.7
  974.3 19.4 all-reduce.1
